TPU v7x, 32 devices: a whole 2x2x4 slice. The times are simulated.
32 devices in a mesh: gx: 4 (over y, core), gy: 8 (over z, x).
Axes of the slice: x: 2, y: 2, z: 4, core: 2. Of those that a mesh axis runs over, the one named last changes fastest.
Arguments:
- disp: float32 [3, 32, 128, 128], P(None, 'gx', 'gy'), may hold values from -3 to 3
- vel: float32 [3, 32, 128, 128], P(None, 'gx', 'gy'), may hold values from -30 to 30
- load: float32 [3, 32, 128, 128], P(None, 'gx', 'gy'), may hold values from -96 to 96
- flags: int32 [32, 128, 128], P('gx', 'gy'), may hold values 0 or 1
- mask_bits: int32 [4, 32, 128, 128], P(None, 'gx', 'gy'), may hold values from 0 to 2147483647, as said below
Outputs:
- disp_out: float32 [3, 32, 128, 128], P(None, 'gx', 'gy')
- vel_out: float32 [3, 32, 128, 128], P(None, 'gx', 'gy')
Inputs may be any that keep to these rules, and one draw needn't show every extreme that they name: `mask_bits`: bit b (0 to 30) of word w marks the cell's bond to neighbour number 31 w + b as broken; bit 31, and bits of numbers 122 and above, are zero.
All inputs are finite; a program needn't handle non-finite values. No bound on the sum of `flags` on one device may be relied on, other than what follows from the above.
Results may differ from a plain program's by a relative error of at most 0.0001.
Values sent between devices are 32-bit elements; how exact they have to be, the bound alone decides.
A program may use at most 128 MiB of HBM per device.

v0:
```python
import functools
import math

import jax
import jax.numpy as jnp
from jax import lax
from jax.experimental import pallas as pl
from jax.experimental.pallas import tpu as pltpu
from jax.sharding import PartitionSpec as P

ITERS = 8
MESH = pl.DeviceIdType.MESH

fictive_mass = 64.0
epsilon = 1e-06

EDGE = 8


def neighbour_table():
    table = []
    for across in range(-3, 4):
        for along in range(-3, 4):
            for upward in range(-3, 4):
                length = across * across + along * along + upward * upward
                if 0 < length <= 9:
                    table.append((across, along, upward))
    return table


TABLE = neighbour_table()
NUMBER = {offset: number for number, offset in enumerate(TABLE)}


def reach(along, upward):
    return [a for a in range(-3, 4) if (a, along, upward) in NUMBER]


def rolled(cells, upward):
    depth = cells.shape[-1]
    if upward == 0:
        return cells
    return pltpu.roll(cells, (-upward) % depth, cells.ndim - 1)


def kernel(
    nx, ny,
    disp, vel, load, flags, mask,
    field, speed,
    weights, diagonal, pad, mask_pad, shifted, mask_shifted, mixed, plain, force, total, change,
    rim_x, rim_y, rim_c, pack_y, pack_c,
    mrim_x, mrim_y, mrim_c, mpack_y, mpack_c,
    sums_out, sums_in,
    send_sem, recv_sem, msend_sem, mrecv_sem, sum_send_sem, sum_recv_sem,
):
    rows, cols, depth = flags.shape
    count = 3.0 * rows * nx * cols * ny * depth
    devices = nx * ny
    my_x = lax.axis_index("gx")
    my_y = lax.axis_index("gy")

    sides = []
    for step_x, step_y in ((-1, 0), (1, 0), (0, -1), (0, 1), (-1, -1), (-1, 1), (1, -1), (1, 1)):
        there = None
        for step, mine, size in ((step_x, my_x, nx), (step_y, my_y, ny)):
            if step:
                near = mine > 0 if step < 0 else mine < size - 1
                there = near if there is None else there & near
        sides.append((step_x, step_y, there))

    def copies(index, source, rims, packs, sems, slot):
        step_x, step_y, there = sides[index]
        target = (my_x + step_x, my_y + step_y)
        if index < 2:
            start = 0 if step_x < 0 else rows - 3
            src = source.at[:, pl.ds(start, 3)]
            dst = rims[0].at[slot, 1 - index]
        elif index < 4:
            src = packs[0].at[slot, index - 2]
            dst = rims[1].at[slot, 3 - index]
        else:
            src = packs[1].at[slot, index - 4]
            dst = rims[2].at[slot, 7 - index]
        return pltpu.make_async_remote_copy(
            src_ref=src, dst_ref=dst,
            send_sem=sems[0].at[slot, index], recv_sem=sems[1].at[slot, index ^ 1 if index < 4 else 11 - index],
            device_id=target, device_id_type=MESH,
        )

    def exchange(source, rims, packs, sems, slot):
        for index in (0, 1):
            @pl.when(sides[index][2])
            def _():
                copies(index, source, rims, packs, sems, slot).start()
        parts = source.shape[0]
        for c in range(parts):
            for j in range(3):
                packs[0][slot, 0, c, j] = source[c, :, j, :]
                packs[0][slot, 1, c, j] = source[c, :, cols - 3 + j, :]
            for corner in range(4):
                step_x, step_y, _ = sides[4 + corner]
                for i in range(2):
                    x = i if step_x < 0 else rows - 2 + i
                    y = 0 if step_y < 0 else cols - 2
                    packs[1][slot, corner, c, pl.ds(2 * i, 2), :] = source[c, x, pl.ds(y, 2), :]
        for index in range(2, 8):
            @pl.when(sides[index][2])
            def _():
                copies(index, source, rims, packs, sems, slot).start()

    def arrive(source, rims, packs, sems, slot, padded):
        parts = source.shape[0]
        for index in range(8):
            step_x, step_y, there = sides[index]

            @pl.when(there)
            def _():
                step = copies(index, source, rims, packs, sems, slot)
                step.wait_send()
                back = copies(index ^ 1 if index < 4 else 11 - index, source, rims, packs, sems, slot)
                back.wait_recv()
                if index < 2:
                    first = 0 if step_x < 0 else 3 + rows
                    padded[:, pl.ds(first, 3), pl.ds(EDGE, cols), :] = rims[0][slot, index]
                elif index < 4:
                    first = EDGE - 3 if step_y < 0 else EDGE + cols
                    for c in range(parts):
                        for j in range(3):
                            padded[c, pl.ds(3, rows), first + j, :] = rims[1][slot, index - 2, c, j]
                else:
                    x = 1 if step_x < 0 else 3 + rows
                    y = EDGE - 2 if step_y < 0 else EDGE + cols
                    for c in range(parts):
                        for i in range(2):
                            padded[c, x + i, pl.ds(y, 2), :] = rims[2][slot, index - 4, c, pl.ds(2 * i, 2), :]

    rims, packs, sems = (rim_x, rim_y, rim_c), (pack_y, pack_c), (send_sem, recv_sem)
    mrims, mpacks, msems = (mrim_x, mrim_y, mrim_c), (mpack_y, mpack_c), (msend_sem, mrecv_sem)

    exchange(mask, mrims, mpacks, msems, 0)
    exchange(vel, rims, packs, sems, 0)
    exchange(disp, rims, packs, sems, 1)

    pad[...] = jnp.zeros_like(pad)
    mask_pad[...] = jnp.full_like(mask_pad, -1)
    mask_pad[:, pl.ds(3, rows), pl.ds(EDGE, cols), :] = mask[...]
    field[...] = disp[...]
    speed[...] = vel[...]
    diagonal[...] = jnp.zeros_like(diagonal)
    arrive(mask, mrims, mpacks, msems, 0, mask_pad)

    place = lax.broadcasted_iota(jnp.int32, (1, 1, depth), 2)
    for along in range(-3, 4):
        for word in range(4):
            mask_shifted[word] = mask_pad[word, :, pl.ds(EDGE + along, cols), :]
        for upward in range(-3, 4):
            across_all = reach(along, upward)
            if not across_all:
                continue
            inside = (place + upward >= 0) & (place + upward < depth)
            for low in range(0, rows, 4):
                moments = [None, None, None]
                for across in across_all:
                    number = NUMBER[(across, along, upward)]
                    word, bit = divmod(number, 31)
                    mirror_word, mirror_bit = divmod(121 - number, 31)
                    length = float(across * across + along * along + upward * upward)
                    weight = 1.0 / (length * math.sqrt(length))
                    own = mask[word, pl.ds(low, 4)] & (1 << bit)
                    far = mask_shifted[mirror_word, pl.ds(3 + low + across, 4)] & (1 << mirror_bit)
                    far = rolled(jnp.where(far == 0, jnp.float32(weight), jnp.float32(0.0)), upward)
                    one = jnp.where((own == 0) & inside, far, jnp.float32(0.0))
                    weights[number, pl.ds(low, 4)] = one
                    for power in range(3):
                        scale = float(across**power)
                        if scale != 0.0:
                            term = one if scale == 1.0 else scale * one
                            moments[power] = term if moments[power] is None else moments[power] + term
                for slot, (power, scale) in enumerate((
                    (2, 1), (1, along), (1, upward), (0, along * along), (0, along * upward), (0, upward * upward),
                )):
                    if scale and moments[power] is not None:
                        diagonal[slot, pl.ds(low, 4)] += float(scale) * moments[power]

    def apply_forces():
        for low in range(0, rows, 4):
            here = pl.ds(low, 4)
            u = [pad[c, pl.ds(3 + low, 4), pl.ds(EDGE, cols), :] for c in range(3)]
            d = [diagonal[slot, here] for slot in range(6)]
            force[0, here] = -(d[0] * u[0] + d[1] * u[1] + d[2] * u[2])
            force[1, here] = -(d[1] * u[0] + d[3] * u[1] + d[4] * u[2])
            force[2, here] = -(d[2] * u[0] + d[4] * u[1] + d[5] * u[2])
        turn = 0
        for along in range(-3, 4):
            for c in range(3):
                shifted[c] = pad[c, :, pl.ds(EDGE + along, cols), :]
            for upward in range(-3, 4):
                across_all = reach(along, upward)
                if not across_all:
                    continue
                turn = 1 - turn
                most = max(across_all)
                span = pl.ds(3 - most, rows + 2 * most)
                if along or upward:
                    mix = None
                    for scale, c in ((along, 1), (upward, 2)):
                        if scale:
                            term = float(scale) * shifted[c, span] if scale != 1 else shifted[c, span]
                            mix = term if mix is None else mix + term
                    mixed[turn, span] = rolled(mix, upward)
                if most:
                    plain[turn, span] = rolled(shifted[0, span], upward)
                for low in range(0, rows, 4):
                    here = pl.ds(low, 4)
                    whole = None
                    lean = None

                    def stretch(across):
                        at = pl.ds(3 + low + across, 4)
                        value = mixed[turn, at] if along or upward else None
                        if across:
                            term = float(across) * plain[turn, at]
                            value = term if value is None else value + term
                        return weights[NUMBER[(across, along, upward)], here] * value

                    for across in [a for a in across_all if a >= 0]:
                        if across == 0:
                            whole = stretch(0)
                            continue
                        up, down = stretch(across), stretch(-across)
                        both = up + down
                        whole = both if whole is None else whole + both
                        gap = float(across) * (up - down) if across != 1 else up - down
                        lean = gap if lean is None else lean + gap
                    if lean is not None:
                        force[0, here] += lean
                    if along:
                        force[1, here] += float(along) * whole
                    if upward:
                        force[2, here] += float(upward) * whole

    me = my_x * ny + my_y

    def send_sums(slot):
        kinetic = jnp.sum(speed[...] * speed[...], axis=(0, 1))
        rayleigh = jnp.sum(speed[...] * change[...], axis=(0, 1))
        sums_out[slot, pl.ds(0, 1), :] = jnp.sum(kinetic, axis=0, keepdims=True)
        sums_out[slot, pl.ds(1, 1), :] = jnp.sum(rayleigh, axis=0, keepdims=True)

        def send(r, carry):
            target = lax.rem(me + 1 + r, devices)
            pltpu.make_async_remote_copy(
                src_ref=sums_out.at[slot], dst_ref=sums_in.at[slot, r],
                send_sem=sum_send_sem.at[slot], recv_sem=sum_recv_sem.at[slot],
                device_id=(target // ny, lax.rem(target, ny)), device_id_type=MESH,
            ).start()
            return carry

        lax.fori_loop(0, devices - 1, send, 0)

    def take_sums(slot):
        whole = sums_in.at[slot]
        pltpu.make_async_copy(whole, whole, sum_send_sem.at[slot]).wait()
        pltpu.make_async_copy(whole, whole, sum_recv_sem.at[slot]).wait()
        both = jnp.sum(sums_in[slot], axis=0) + sums_out[slot]
        both = jnp.sum(both, axis=1, keepdims=True)
        kinetic = both[0:1]
        rayleigh = -both[1:2]
        damping = 2.0 * jnp.sqrt(rayleigh / count / (fictive_mass * (kinetic / count + epsilon)))
        alpha = (2.0 - damping) / (2.0 + damping)
        beta = 2.0 / (fictive_mass * (2.0 + damping))
        return alpha[None, None], beta[None, None]

    def advance(alpha, beta):
        for c in range(3):
            speed[c] = alpha[0] * speed[c] + beta[0] * total[c]
            field[c] = field[c] + speed[c]

    middle = (slice(None), pl.ds(3, rows), pl.ds(EDGE, cols), slice(None))

    def step(turn, carry):
        slot = jnp.where(turn < 2, turn, 2 + lax.rem(turn, 2))

        @pl.when(turn == 0)
        def _():
            pad[middle] = vel[...]

        @pl.when(turn == 1)
        def _():
            pad[middle] = disp[...]

        @pl.when(turn >= 2)
        def _():
            pad[middle] = total[...]

        arrive(total, rims, packs, sems, slot, pad)
        apply_forces()

        @pl.when(turn == 0)
        def _():
            change[...] = force[...]
            send_sums(0)

        @pl.when(turn == 1)
        def _():
            for c in range(3):
                total[c] = force[c] + flags[...].astype(jnp.float32) * load[c]
            exchange(total, rims, packs, sems, 2)

        @pl.when(turn >= 2)
        def _():
            alpha, beta = take_sums(lax.rem(turn, 2))
            advance(alpha, beta)
            for c in range(3):
                change[c] = alpha[0] * change[c] + beta[0] * force[c]
                total[c] = total[c] + change[c]

            @pl.when(turn < ITERS)
            def _():
                exchange(total, rims, packs, sems, 2 + lax.rem(turn + 1, 2))

            send_sums(lax.rem(turn + 1, 2))

        return carry

    lax.fori_loop(0, ITERS + 1, step, 0)
    alpha, beta = take_sums((ITERS + 1) % 2)
    advance(alpha, beta)


def on_device(nx, ny, disp, vel, load, flags, mask_bits):
    parts, rows, cols, depth = disp.shape
    words = mask_bits.shape[0]
    f32, i32 = jnp.float32, jnp.int32
    vmem, dma = pltpu.VMEM, pltpu.SemaphoreType.DMA
    wide = cols + 2 * EDGE
    block = (parts, rows, cols, depth)
    scratch = [
        vmem((len(TABLE), rows, cols, depth), f32),
        vmem((6, rows, cols, depth), f32),
        vmem((parts, rows + 6, wide, depth), f32),
        vmem((words, rows + 6, wide, depth), i32),
        vmem((parts, rows + 6, cols, depth), f32),
        vmem((words, rows + 6, cols, depth), i32),
        vmem((2, rows + 6, cols, depth), f32),
        vmem((2, rows + 6, cols, depth), f32),
        vmem(block, f32),
        vmem(block, f32),
        vmem(block, f32),
        vmem((4, 2, parts, 3, cols, depth), f32),
        vmem((4, 2, parts, 3, rows, depth), f32),
        vmem((4, 4, parts, 4, depth), f32),
        vmem((4, 2, parts, 3, rows, depth), f32),
        vmem((4, 4, parts, 4, depth), f32),
        vmem((1, 2, words, 3, cols, depth), i32),
        vmem((1, 2, words, 3, rows, depth), i32),
        vmem((1, 4, words, 4, depth), i32),
        vmem((1, 2, words, 3, rows, depth), i32),
        vmem((1, 4, words, 4, depth), i32),
        vmem((2, 2, depth), f32),
        vmem((2, nx * ny - 1, 2, depth), f32),
        dma((4, 8)),
        dma((4, 8)),
        dma((1, 8)),
        dma((1, 8)),
        dma((2,)),
        dma((2,)),
    ]
    return pl.pallas_call(
        functools.partial(kernel, nx, ny),
        out_shape=[jax.ShapeDtypeStruct(block, f32)] * 2,
        in_specs=[pl.BlockSpec(memory_space=vmem)] * 5,
        out_specs=[pl.BlockSpec(memory_space=vmem)] * 2,
        scratch_shapes=scratch,
        compiler_params=pltpu.CompilerParams(has_side_effects=True, vmem_limit_bytes=48 * 1024 * 1024),
    )(disp, vel, load, flags, mask_bits)


def solution(mesh):
    cells = P(None, "gx", "gy", None)
    return jax.shard_map(
        functools.partial(on_device, mesh.shape["gx"], mesh.shape["gy"]),
        mesh=mesh,
        in_specs=(cells, cells, cells, P("gx", "gy", None), cells),
        out_specs=(cells, cells),
        check_vma=False,
    )
```

profile of v0, /device:TPU:0, one launch (start us, length us, event | category | flops | bytes accessed | tf_op | source)
XLA Modules:
  0.0 77.2 jit_solution(1268630567992296506)
XLA Ops:
  0.6 0.0 copy-start
  0.6 0.9 %copy-done = s32[4,8,16,128]{3,2,1,0:T(8,128)S(1)} copy-done((s32[4,8,16,128]{3,2,1,0:T(8,128)S(1)}, s32[4,8,16,128]{3,2,1,0:T(8,128)}, u32[]{:S(2)}) %copy-start) | copy-done | bytes 262168
  1.6 0.0 copy-start.1
  1.6 0.9 %copy-done.1 = f32[3,8,16,128]{3,2,1,0:T(8,128)S(1)} copy-done((f32[3,8,16,128]{3,2,1,0:T(8,128)S(1)}, f32[3,8,16,128]{3,2,1,0:T(8,128)}, u32[]{:S(2)}) %copy-start.1) | copy-done | bytes 196632
  2.5 0.0 copy-start.2
  2.5 0.9 %copy-done.2 = f32[3,8,16,128]{3,2,1,0:T(8,128)S(1)} copy-done((f32[3,8,16,128]{3,2,1,0:T(8,128)S(1)}, f32[3,8,16,128]{3,2,1,0:T(8,128)}, u32[]{:S(2)}) %copy-start.2) | copy-done | bytes 196632
  3.4 0.0 copy-start.3
  3.4 0.9 %copy-done.3 = f32[3,8,16,128]{3,2,1,0:T(8,128)S(1)} copy-done((f32[3,8,16,128]{3,2,1,0:T(8,128)S(1)}, f32[3,8,16,128]{3,2,1,0:T(8,128)}, u32[]{:S(2)}) %copy-start.3) | copy-done | bytes 196632
  4.4 0.0 copy-start.4
  4.4 0.8 %copy-done.4 = s32[8,16,128]{2,1,0:T(8,128)S(1)} copy-done((s32[8,16,128]{2,1,0:T(8,128)S(1)}, s32[8,16,128]{2,1,0:T(8,128)}, u32[]{:S(2)}) %copy-start.4) | copy-done | bytes 65560
  5.2 70.7 %shard_map.68 = (f32[3,8,16,128]{3,2,1,0:T(8,128)S(1)}, f32[3,8,16,128]{3,2,1,0:T(8,128)S(1)}) custom-call(f32[3,8,16,128]{3,2,1,0:T(8,128)S(1)} %copy-done.1, f32[3,8,16,128]{3,2,1,0:T(8,128)S(1)} %copy-done.2, f32[3,8,16,128]{3,2,1,0:T(8,128)S(1)} %copy-done.3, s32[8,16,128]{2,1,0:T(8,128)S(1)} %copy-done.4, s32[4,8,16,128]{3,2,1,0:T(8,128)S(1)} %copy-done), custom_call_target="tpu_custom_call" | custom-call | tf_op jit(solution)/shard_map/pallas_call | solution.py:369
  75.9 0.7 copy.9
  76.6 0.7 copy.10
Async XLA Ops:
  0.6 1.0 %copy-start = (s32[4,8,16,128]{3,2,1,0:T(8,128)S(1)}, s32[4,8,16,128]{3,2,1,0:T(8,128)}, u32[]{:S(2)}) copy-start(s32[4,8,16,128]{3,2,1,0:T(8,128)} %mask.1) | copy-start | bytes 786436
  1.6 0.9 %copy-start.1 = (f32[3,8,16,128]{3,2,1,0:T(8,128)S(1)}, f32[3,8,16,128]{3,2,1,0:T(8,128)}, u32[]{:S(2)}) copy-start(f32[3,8,16,128]{3,2,1,0:T(8,128)} %disp.1) | copy-start | bytes 589828
  2.5 0.9 %copy-start.2 = (f32[3,8,16,128]{3,2,1,0:T(8,128)S(1)}, f32[3,8,16,128]{3,2,1,0:T(8,128)}, u32[]{:S(2)}) copy-start(f32[3,8,16,128]{3,2,1,0:T(8,128)} %vel.1) | copy-start | bytes 589828
  3.4 0.9 %copy-start.3 = (f32[3,8,16,128]{3,2,1,0:T(8,128)S(1)}, f32[3,8,16,128]{3,2,1,0:T(8,128)}, u32[]{:S(2)}) copy-start(f32[3,8,16,128]{3,2,1,0:T(8,128)} %load.1) | copy-start | bytes 589828
  4.4 0.8 %copy-start.4 = (s32[8,16,128]{2,1,0:T(8,128)S(1)}, s32[8,16,128]{2,1,0:T(8,128)}, u32[]{:S(2)}) copy-start(s32[8,16,128]{2,1,0:T(8,128)} %flags.1) | copy-start | bytes 196612
where the time goes:
time: 77.5 us; the launch traced here: 77.2 us
  Pallas kernels  70.7 us (91%)
  local copies, waits for them, and re-layouts  5.92 us (8%)
    pallas_call x1, Pallas kernels, on_device(): pl.pallas_call(functools.partial(kernel, nx, ny), out_shape=[jax.ShapeDty...  70.7 us
    unnamed x12, local copies, waits for them, and re-layouts  5.92 us

commit v1 on v0

v1 whole, which is shorter than its diff:
```python
import functools
import math

import jax
import jax.numpy as jnp
from jax import lax
from jax.experimental import pallas as pl
from jax.experimental.pallas import tpu as pltpu
from jax.sharding import PartitionSpec as P

ITERS = 8
MESH = pl.DeviceIdType.MESH

fictive_mass = 64.0
epsilon = 1e-06

EDGE = 8
SLOTS = 4


def neighbour_table():
    table = []
    for across in range(-3, 4):
        for along in range(-3, 4):
            for upward in range(-3, 4):
                length = across * across + along * along + upward * upward
                if 0 < length <= 9:
                    table.append((across, along, upward))
    return table


TABLE = neighbour_table()
NUMBER = {offset: number for number, offset in enumerate(TABLE)}

PLANES = [(1, 0), (1, 1), (2, 0)]
LONG = [(1, 2), (2, 1), (3, 0)]


def reach(along, upward):
    return [a for a in range(-3, 4) if (a, along, upward) in NUMBER]


def crossing(layer, r):
    far = layer + r
    return [(p, c) for c in range(-2, 3) for p in range(-2, 3) if far * far + p * p + c * c <= 9]


FACE = {}
for plane in PLANES:
    for offset in crossing(*plane):
        FACE[plane + offset] = len(FACE)
for plane in LONG:
    FACE[plane + (0, 0)] = len(FACE)


def bond(offset):
    number = NUMBER[offset]
    word, bit = divmod(number, 31)
    mirror_word, mirror_bit = divmod(121 - number, 31)
    length = float(sum(part * part for part in offset))
    return word, 1 << bit, mirror_word, 1 << mirror_bit, 1.0 / (length * math.sqrt(length))


def rolled(cells, upward):
    depth = cells.shape[-1]
    if upward == 0:
        return cells
    return pltpu.roll(cells, (-upward) % depth, cells.ndim - 1)


def add(total, term):
    return term if total is None else total + term


def scaled(scale, value):
    return value if scale == 1 else float(scale) * value


def kernel(
    nx, ny,
    disp_in, vel_in, load_in, flags_in, mask_in,
    field, speed,
    load, flags, mask,
    weights, diagonal, pad, mask_pad, shifted, mask_shifted, mixed, plain, force, total, change,
    wx, wy, xg, xw, yg, yw, xr, yr, mxr, myr, mx3, my3,
    xpack, ypack, xslot, yslot, mxpack, mypack, my3pack, mxslot, myslot, my3slot,
    acc, ab, sums_out, sums_in,
    local_sem, send_sem, recv_sem, msend_sem, mrecv_sem, sum_send_sem, sum_recv_sem, ready,
):
    depth = flags.shape[-1]
    cells = flags.shape[0]
    rows = pad.shape[1] - 6
    cols = cells // rows
    count = 3.0 * rows * nx * cols * ny * depth
    devices = nx * ny
    my_x = lax.axis_index("gx")
    my_y = lax.axis_index("gy")
    f32, i32 = jnp.float32, jnp.int32

    fetches = [
        pltpu.make_async_copy(src, dst, local_sem.at[index])
        for index, (src, dst) in enumerate((
            (mask_in, mask), (disp_in, field), (vel_in, speed), (load_in, load), (flags_in, flags),
        ))
    ]
    for fetch in fetches:
        fetch.start()

    sides = []
    for step_x, step_y in ((-1, 0), (1, 0), (0, -1), (0, 1), (-1, -1), (-1, 1), (1, -1), (1, 1)):
        there = None
        for step, mine, size in ((step_x, my_x, nx), (step_y, my_y, ny)):
            if step:
                near = mine > 0 if step < 0 else mine < size - 1
                there = near if there is None else there & near
        sides.append((step_x, step_y, there))

    barrier = pltpu.get_barrier_semaphore()
    peers = nx + ny - 2
    for step_x, step_y, there in sides[4:]:
        @pl.when(there)
        def _():
            pl.semaphore_signal(barrier, inc=1, device_id=(my_x + step_x, my_y + step_y), device_id_type=MESH)
        peers = peers + there.astype(i32)
    for hop in range(1, ny):
        pl.semaphore_signal(barrier, inc=1, device_id=(my_x, lax.rem(my_y + hop, ny)), device_id_type=MESH)
    for hop in range(1, nx):
        pl.semaphore_signal(barrier, inc=1, device_id=(lax.rem(my_x + hop, nx), my_y), device_id_type=MESH)

    def opposite(index):
        return index ^ 1 if index < 4 else 11 - index

    def outgoing(index, slot):
        step_x, step_y, _ = sides[index]
        if index < 2:
            src, dst = xpack.at[slot, index], xslot.at[slot, 1 - index]
        elif index < 4:
            src, dst = ypack.at[slot, index - 2], yslot.at[slot, 3 - index, pl.ds(2 * 8, rows * 8)]
        else:
            side = 0 if step_y < 0 else 1
            start = 0 if step_x < 0 else rows - 2
            land = rows + 2 if step_x < 0 else 0
            src = ypack.at[slot, side, pl.ds(start * 8, 16)]
            dst = yslot.at[slot, 1 - side, pl.ds(land * 8, 16)]
        return pltpu.make_async_remote_copy(
            src_ref=src, dst_ref=dst, send_sem=send_sem.at[slot, index], recv_sem=recv_sem.at[slot, opposite(index)],
            device_id=(my_x + step_x, my_y + step_y), device_id_type=MESH,
        )

    def outgoing_mask(index):
        step_x, step_y, _ = sides[index]
        if index < 2:
            pairs = [(mxpack.at[index], mxslot.at[1 - index])]
        elif index < 4:
            pairs = [
                (mypack.at[index - 2], myslot.at[3 - index, pl.ds(2 * 8, rows * 8)]),
                (my3pack.at[index - 2], my3slot.at[3 - index]),
            ]
        else:
            side = 0 if step_y < 0 else 1
            start = 0 if step_x < 0 else rows - 2
            land = rows + 2 if step_x < 0 else 0
            pairs = [(mypack.at[side, pl.ds(start * 8, 16)], myslot.at[1 - side, pl.ds(land * 8, 16)])]
        return [
            pltpu.make_async_remote_copy(
                src_ref=src, dst_ref=dst, send_sem=msend_sem.at[part, index],
                recv_sem=mrecv_sem.at[part, opposite(index)],
                device_id=(my_x + step_x, my_y + step_y), device_id_type=MESH,
            )
            for part, (src, dst) in enumerate(pairs)
        ]

    ORDER = (4, 5, 6, 7, 2, 3, 0, 1)

    def column(at):
        return pl.ds(at, rows, stride=cols)

    def spread(at):
        return pl.ds(at, rows, stride=8)

    def pack(source, slot):
        for side in range(2):
            for layer in (1, 2, 3):
                at = layer - 1 if side == 0 else cols - layer
                for c in range(3) if layer < 3 else (1,):
                    e = 3 * (layer - 1) + (c if layer < 3 else 0)
                    ypack[slot, side, spread(e), :] = source[c, column(at), :]
        for index in ORDER[:6]:
            @pl.when(sides[index][2])
            def _():
                outgoing(index, slot).start()
        for side in range(2):
            for layer in (1, 2, 3):
                at = layer - 1 if side == 0 else rows - layer
                for c in range(3) if layer < 3 else (0,):
                    e = 3 * (layer - 1) + c
                    xpack[slot, side, pl.ds(e * cols, cols), :] = source[c, pl.ds(at * cols, cols), :]
        for index in ORDER[6:]:
            @pl.when(sides[index][2])
            def _():
                outgoing(index, slot).start()

    def arrived(index, slot):
        outgoing(index, slot).wait_send()
        outgoing(opposite(index), slot).wait_recv()

    pad[...] = jnp.zeros_like(pad)
    mask_pad[...] = jnp.full_like(mask_pad, -1)
    diagonal[...] = jnp.zeros_like(diagonal)
    for state in (xg, xw, yg, yw, xr, ypack, acc):
        state[...] = jnp.zeros_like(state)
    for state in (mxr, myr, mx3, my3, mypack):
        state[...] = jnp.full_like(state, -1)
    ab[...] = jnp.where(lax.broadcasted_iota(i32, ab.shape, 0) == 0, 1.0, 0.0).astype(f32)
    place = lax.broadcasted_iota(i32, (1, depth), 1)
    fetches[0].wait()
    for word in range(4):
        for r in range(rows):
            mask_pad[word, 3 + r, pl.ds(EDGE, cols), :] = mask[word, pl.ds(r * cols, cols), :]

    for along in range(-3, 4):
        for word in range(4):
            mask_shifted[word] = mask_pad[word, :, pl.ds(EDGE + along, cols), :].reshape(-1, depth)
        for upward in range(-3, 4):
            across_all = reach(along, upward)
            if not across_all:
                continue
            inside = (place + upward >= 0) & (place + upward < depth)
            for low in range(0, rows, 4):
                here = pl.ds(low * cols, 4 * cols)
                moments = [None, None, None]
                for across in across_all:
                    word, bit, mirror_word, mirror_bit, weight = bond((across, along, upward))
                    own = mask[word, here] & bit
                    far = mask_shifted[mirror_word, pl.ds((3 + low + across) * cols, 4 * cols)] & mirror_bit
                    far = rolled(jnp.where(far == 0, f32(weight), f32(0.0)), upward)
                    one = jnp.where((own == 0) & inside, far, f32(0.0))
                    weights[NUMBER[(across, along, upward)], here] = one
                    for power in range(3):
                        scale = across**power
                        if scale:
                            moments[power] = add(moments[power], scaled(scale, one))
                for slot, (power, scale) in enumerate((
                    (2, 1), (1, along), (1, upward), (0, along * along), (0, along * upward), (0, upward * upward),
                )):
                    if scale and moments[power] is not None:
                        diagonal[slot, here] += scaled(scale, moments[power])

    for side in range(2):
        for layer in (1, 2):
            at = layer - 1 if side == 0 else cols - layer
            for word in range(4):
                mypack[side, spread(4 * (layer - 1) + word), :] = mask[word, column(at), :]
            at = layer - 1 if side == 0 else rows - layer
            for word in range(4):
                e = 4 * (layer - 1) + word
                mxpack[side, pl.ds(e * cols, cols), :] = mask[word, pl.ds(at * cols, cols), :]
        sign = 1 if side == 0 else -1
        word = bond((0, 3 * sign, 0))[2]
        my3pack[side] = mask[word, column(2 if side == 0 else cols - 3), :]
        word = bond((3 * sign, 0, 0))[2]
        mxpack[side, pl.ds(8 * cols, cols), :] = mask[word, pl.ds((2 if side == 0 else rows - 3) * cols, cols), :]

    pl.semaphore_wait(barrier, peers)
    for hop in range(1, ny):
        pl.semaphore_signal(ready, inc=1, device_id=(my_x, lax.rem(my_y + hop, ny)), device_id_type=MESH)
    for index in ORDER:
        @pl.when(sides[index][2])
        def _():
            for copy in outgoing_mask(index):
                copy.start()
    fetches[1].wait()
    pack(field, 0)
    fetches[2].wait()
    pack(speed, 1)

    middle = (slice(None), pl.ds(3, rows), pl.ds(EDGE, cols), slice(None))

    def set_pad(c, value):
        pad[c, pl.ds(3, rows), pl.ds(EDGE, cols), :] = value.reshape(rows, cols, depth)

    for c in range(3):
        set_pad(c, field[c])

    def face_weights(side):
        sign = -1 if side == 0 else 1
        for axis in (0, 1):
            terms = {}
            for layer, r in PLANES + LONG:
                for p, c in crossing(layer, r) if (layer, r) in PLANES else [(0, 0)]:
                    out = sign * (layer + r)
                    offset = (out, p, c) if axis == 0 else (p, out, c)
                    word, bit, mirror_word, mirror_bit, weight = bond(offset)
                    if axis == 0:
                        at = r if side == 0 else rows - 1 - r
                        own = mask[word, pl.ds(at * cols, cols), :]
                        if layer == 3:
                            far = mx3[side]
                        else:
                            far = mxr[side, c + 2, 4 * (layer - 1) + mirror_word, pl.ds(EDGE + p, cols), :]
                    else:
                        at = r if side == 0 else cols - 1 - r
                        own = mask[word, column(at), :]
                        if layer == 3:
                            far = my3[side]
                        else:
                            far = myr[side, c + 2, spread((2 + p) * 8 + 4 * (layer - 1) + mirror_word), :]
                    one = jnp.where(((own & bit) | (far & mirror_bit)) == 0, f32(weight), f32(0.0))
                    if axis == 0:
                        wx[side, FACE[layer, r, p, c]] = one
                    else:
                        wy[side, FACE[layer, r, p, c]] = one
                    slot = 0
                    for i in range(3):
                        for j in range(i, 3):
                            scale = offset[i] * offset[j]
                            if scale:
                                key = (r, slot)
                                terms[key] = add(terms.get(key), scaled(scale, one))
                            slot += 1
            for (r, slot), term in terms.items():
                if axis == 0:
                    at = r if side == 0 else rows - 1 - r
                    diagonal[slot, pl.ds(at * cols, cols), :] += term
                else:
                    at = r if side == 0 else cols - 1 - r
                    diagonal[slot, column(at), :] += term

    def take_masks():
        for index in range(8):
            step_x, step_y, there = sides[index]

            @pl.when(there)
            def _():
                for copy in outgoing_mask(index):
                    copy.wait_send()
                for copy in outgoing_mask(opposite(index)):
                    copy.wait_recv()
                for upward in range(-2, 3):
                    inside = (place + upward >= 0) & (place + upward < depth)
                    if index < 2:
                        words = mxslot[index, pl.ds(0, 8 * cols), :]
                    elif index < 4:
                        first, size = 2 * 8, rows * 8
                        words = myslot[index - 2, pl.ds(first, size), :]
                    else:
                        first, size = (0 if step_x < 0 else (rows + 2) * 8), 16
                        words = myslot[0 if step_y < 0 else 1, pl.ds(first, size), :]
                    if upward:
                        words = jnp.where(inside, rolled(words, upward), -1)
                    if index < 2:
                        mxr[index, upward + 2, :, pl.ds(EDGE, cols), :] = words.reshape(8, cols, depth)
                    else:
                        myr[0 if step_y < 0 else 1, upward + 2, pl.ds(first, size), :] = words
                if index < 2:
                    mx3[index] = mxslot[index, pl.ds(8 * cols, cols), :]
                elif index < 4:
                    my3[index - 2] = my3slot[index - 2]
        for side in range(2):
            face_weights(side)

    def own_forces():
        turn = 0
        for low in range(0, rows, 4):
            for c in range(3):
                force[c, pl.ds(low * cols, 4 * cols)] = jnp.zeros((4 * cols, depth), f32)
        for along in range(-3, 4):
            for c in range(3):
                shifted[c] = pad[c, :, pl.ds(EDGE + along, cols), :].reshape(-1, depth)
            for upward in range(-3, 4):
                across_all = reach(along, upward)
                if not across_all:
                    continue
                turn = 1 - turn
                most = max(across_all)
                span = pl.ds(3 * cols, rows * cols)
                if along or upward:
                    mix = None
                    for scale, c in ((along, 1), (upward, 2)):
                        if scale:
                            mix = add(mix, scaled(scale, shifted[c, span]))
                    mixed[turn, span] = rolled(mix, upward)
                if most:
                    plain[turn, span] = rolled(shifted[0, span], upward)
                for low in range(0, rows, 4):
                    here = pl.ds(low * cols, 4 * cols)
                    whole = None
                    lean = None

                    def stretch(across):
                        at = pl.ds((3 + low + across) * cols, 4 * cols)
                        value = mixed[turn, at] if along or upward else None
                        if across:
                            term = float(across) * plain[turn, at]
                            value = term if value is None else value + term
                        return weights[NUMBER[(across, along, upward)], here] * value

                    for across in [a for a in across_all if a >= 0]:
                        if across == 0:
                            whole = stretch(0)
                            continue
                        up, down = stretch(across), stretch(-across)
                        both = up + down
                        whole = both if whole is None else whole + both
                        lean = add(lean, scaled(across, up - down))
                    if lean is not None:
                        force[0, here] += lean
                    if along:
                        force[1, here] += float(along) * whole
                    if upward:
                        force[2, here] += float(upward) * whole

    def diagonal_forces():
        for low in range(0, rows, 4):
            here = pl.ds(low * cols, 4 * cols)
            u = [pad[c, pl.ds(3 + low, 4), pl.ds(EDGE, cols), :].reshape(4 * cols, depth) for c in range(3)]
            d = [diagonal[slot, here] for slot in range(6)]
            force[0, here] -= d[0] * u[0] + d[1] * u[1] + d[2] * u[2]
            force[1, here] -= d[1] * u[0] + d[3] * u[1] + d[4] * u[2]
            force[2, here] -= d[2] * u[0] + d[4] * u[1] + d[5] * u[2]

    def face_forces(axis, side):
        sign = -1 if side == 0 else 1
        normal, tangent = (0, 1) if axis == 0 else (1, 0)
        result = {}
        for layer in (1, 2):
            inner = [r for one, r in PLANES if one == layer]
            wide = {}
            for c in range(-2, 3):
                sums = {}
                for p in range(-2, 3):
                    targets = [r for r in inner if (layer, r, p, c) in FACE]
                    if not targets:
                        continue

                    def near(component):
                        e = 3 * (layer - 1) + component
                        if axis == 0:
                            return xr[side, c + 2, e, pl.ds(EDGE + p, cols), :]
                        return yr[side, c + 2, spread((2 + p) * 8 + e), :]

                    out = near(normal)
                    base = None
                    if p:
                        base = scaled(p, near(tangent))
                    if c:
                        base = add(base, scaled(c, near(2)))
                    for r in targets:
                        value = scaled(sign * (layer + r), out)
                        if base is not None:
                            value = value + base
                        one = (wx if axis == 0 else wy)[side, FACE[layer, r, p, c]] * value
                        sums[r, 0] = add(sums.get((r, 0)), one)
                        if p:
                            sums[r, 1] = add(sums.get((r, 1)), scaled(p, one))
                for r in inner:
                    if (r, 0) not in sums:
                        continue
                    wide[r, normal] = add(wide.get((r, normal)), sums[r, 0])
                    if (r, 1) in sums:
                        wide[r, tangent] = add(wide.get((r, tangent)), sums[r, 1])
                    if c:
                        wide[r, 2] = add(wide.get((r, 2)), scaled(c, sums[r, 0]))
            for r in inner:
                wide[r, normal] = scaled(sign * (layer + r), wide[r, normal])
                for component in range(3):
                    result[r, component] = add(result.get((r, component)), wide[r, component])
        for layer, r in LONG:
            e = 6 if layer == 3 else 3 * (layer - 1) + normal
            if axis == 0:
                out = xg[side, pl.ds(e * cols, cols), :]
            else:
                out = yg[side, spread(2 * 8 + e), :]
            one = 9.0 * ((wx if axis == 0 else wy)[side, FACE[layer, r, 0, 0]] * out)
            result[r, normal] = add(result.get((r, normal)), one)
        for (r, component), term in result.items():
            if axis == 0:
                at = r if side == 0 else rows - 1 - r
                force[component, pl.ds(at * cols, cols), :] += term
            else:
                at = r if side == 0 else cols - 1 - r
                force[component, column(at), :] += term

    me = my_x * ny + my_y

    def dot(first, second):
        whole = None
        for c in range(3):
            whole = add(whole, jnp.sum((first[c] * second[c]).reshape(-1, 8, depth), axis=0))
        return whole

    def send_sums(slot):
        line = jnp.zeros((1, depth), f32)
        for which in range(6):
            one = jnp.sum(jnp.sum(acc[which], axis=0, keepdims=True), axis=1, keepdims=True)
            line = jnp.where(place == which, one, line)
        sums_out[slot] = line

        def send(r, carry):
            target = lax.rem(me + 1 + r, devices)
            pltpu.make_async_remote_copy(
                src_ref=sums_out.at[slot], dst_ref=sums_in.at[slot, r],
                send_sem=sum_send_sem.at[slot], recv_sem=sum_recv_sem.at[slot],
                device_id=(target // ny, lax.rem(target, ny)), device_id_type=MESH,
            ).start()
            return carry

        lax.fori_loop(0, devices - 1, send, 0)

    def take_sums(slot):
        whole = sums_in.at[slot]
        pltpu.make_async_copy(whole, whole, sum_send_sem.at[slot]).wait()
        pltpu.make_async_copy(whole, whole, sum_recv_sem.at[slot]).wait()
        line = jnp.sum(sums_in[slot], axis=0) + sums_out[slot]
        vv, vg, gg, vw, wg, gh = [
            jnp.sum(jnp.where(place == which, line, 0.0), axis=1, keepdims=True) for which in range(6)
        ]
        alpha, beta = ab[0:1, 0:1], ab[1:2, 0:1]
        kinetic = alpha * alpha * vv + 2.0 * alpha * beta * vg + beta * beta * gg
        rayleigh = -(alpha * alpha * vw + 2.0 * alpha * beta * wg + beta * beta * gh)
        damping = 2.0 * jnp.sqrt(rayleigh / count / (fictive_mass * (kinetic / count + epsilon)))
        alpha = (2.0 - damping) / (2.0 + damping)
        beta = 2.0 / (fictive_mass * (2.0 + damping))
        ab[0:1, :] = jnp.broadcast_to(alpha, (1, depth))
        ab[1:2, :] = jnp.broadcast_to(beta, (1, depth))
        return alpha, beta

    def step(turn, carry):
        own_forces()

        @pl.when(turn == 0)
        def _():
            take_masks()

        diagonal_forces()

        slot = jnp.where(turn < 3, turn, lax.rem(turn + 1, SLOTS))
        early = turn < 3
        alpha = jnp.where(early, 0.0, ab[0:1, :])
        beta = jnp.where(early, 1.0, ab[1:2, :])
        keep = jnp.where(early, 0.0, jnp.ones((1, depth), f32))

        @pl.when(turn == 3)
        def _():
            for index in range(8):
                step_x, step_y, there = sides[index]

                @pl.when(there)
                def _():
                    arrived(index, 3)
                    if index < 2:
                        xw[index] = xslot[3, index]
                    else:
                        side = 0 if step_y < 0 else 1
                        here = pl.ds(16, rows * 8) if index < 4 else pl.ds(0 if step_x < 0 else (rows + 2) * 8, 16)
                        yw[side, here] = yslot[3, side, here]

        for index in (0, 1):
            @pl.when(sides[index][2])
            def _():
                arrived(index, slot)
                fresh = alpha * xw[index] + beta * xslot[slot, index]
                xw[index] = fresh
                fresh = keep * xg[index] + fresh
                xg[index] = fresh
                for upward in range(-2, 3):
                    xr[index, upward + 2, :, pl.ds(EDGE, cols), :] = rolled(
                        fresh[: 6 * cols], upward).reshape(6, cols, depth)
        for side in range(2):
            face_forces(0, side)
        for index in range(2, 8):
            step_x, step_y, there = sides[index]

            @pl.when(there)
            def _():
                arrived(index, slot)
                side = 0 if step_y < 0 else 1
                here = pl.ds(16, rows * 8) if index < 4 else pl.ds(0 if step_x < 0 else (rows + 2) * 8, 16)
                fresh = alpha * yw[side, here] + beta * yslot[slot, side, here]
                yw[side, here] = fresh
                yg[side, here] = keep * yg[side, here] + fresh
        for side in range(2):
            for upward in range(-2, 3):
                yr[side, upward + 2] = rolled(yg[side], upward)
        for side in range(2):
            face_forces(1, side)

        @pl.when(turn == 0)
        def _():
            fetches[3].wait()
            fetches[4].wait()
            for c in range(3):
                whole = force[c] + flags[...].astype(f32) * load[c]
                force[c] = whole
                total[c] = whole

        @pl.when(turn < ITERS)
        def _():
            pack(force, lax.rem(turn + 2, SLOTS))

        @pl.when(turn == 0)
        def _():
            for c in range(3):
                set_pad(c, speed[c])

        @pl.when(turn == 1)
        def _():
            for c in range(3):
                change[c] = force[c]
                set_pad(c, total[c])
            acc[0] = dot(speed, speed)
            acc[1] = dot(speed, total)
            acc[2] = dot(total, total)
            acc[3] = dot(speed, force)
            acc[4] = dot(force, total)
            pl.semaphore_wait(ready, ny - 1)
            send_sums(0)

        @pl.when(turn >= 2)
        def _():
            acc[5] = dot(total, force)
            send_sums(lax.rem(turn - 1, SLOTS))
            alpha, beta = take_sums(lax.rem(turn - 2, SLOTS))
            sums = [None] * 5
            for c in range(3):
                w = alpha * change[c] + beta * force[c]
                v = alpha * speed[c] + beta * total[c]
                g = total[c] + w
                change[c] = w
                speed[c] = v
                total[c] = g
                field[c] = field[c] + v
                set_pad(c, g)
                for which, (a, b) in enumerate(((v, v), (v, g), (g, g), (v, w), (w, g))):
                    sums[which] = add(sums[which], jnp.sum((a * b).reshape(-1, 8, depth), axis=0))
            for which in range(5):
                acc[which] = sums[which]

        return carry

    lax.fori_loop(0, ITERS + 1, step, 0)
    alpha, beta = take_sums((ITERS - 1) % SLOTS)
    for c in range(3):
        v = alpha * speed[c] + beta * total[c]
        speed[c] = v
        field[c] = field[c] + v


def on_device(nx, ny, disp, vel, load, flags, mask_bits):
    parts, rows, cols, depth = disp.shape
    words = mask_bits.shape[0]
    cells = rows * cols
    f32, i32 = jnp.float32, jnp.int32
    vmem, dma = pltpu.VMEM, pltpu.SemaphoreType.DMA
    wide = cols + 2 * EDGE
    flat = (parts, cells, depth)
    tall = (rows + 6) * cols
    ring = (rows + 4) * 8
    scratch = [
        vmem(flat, f32),
        vmem((cells, depth), i32),
        vmem((words, cells, depth), i32),
        vmem((len(TABLE), cells, depth), f32),
        vmem((6, cells, depth), f32),
        vmem((parts, rows + 6, wide, depth), f32),
        vmem((words, rows + 6, wide, depth), i32),
        vmem((parts, tall, depth), f32),
        vmem((words, tall, depth), i32),
        vmem((2, tall, depth), f32),
        vmem((2, tall, depth), f32),
        vmem(flat, f32),
        vmem(flat, f32),
        vmem(flat, f32),
        vmem((2, len(FACE), cols, depth), f32),
        vmem((2, len(FACE), rows, depth), f32),
        vmem((2, 7 * cols, depth), f32),
        vmem((2, 7 * cols, depth), f32),
        vmem((2, ring, depth), f32),
        vmem((2, ring, depth), f32),
        vmem((2, 5, 6, wide, depth), f32),
        vmem((2, 5, ring, depth), f32),
        vmem((2, 5, 8, wide, depth), i32),
        vmem((2, 5, ring, depth), i32),
        vmem((2, cols, depth), i32),
        vmem((2, rows, depth), i32),
        vmem((SLOTS, 2, 7 * cols, depth), f32),
        vmem((SLOTS, 2, rows * 8, depth), f32),
        vmem((SLOTS, 2, 7 * cols, depth), f32),
        vmem((SLOTS, 2, ring, depth), f32),
        vmem((2, 9 * cols, depth), i32),
        vmem((2, rows * 8, depth), i32),
        vmem((2, rows, depth), i32),
        vmem((2, 9 * cols, depth), i32),
        vmem((2, ring, depth), i32),
        vmem((2, rows, depth), i32),
        vmem((6, 8, depth), f32),
        vmem((8, depth), f32),
        vmem((SLOTS, 1, depth), f32),
        vmem((SLOTS, nx * ny - 1, 1, depth), f32),
        dma((5,)),
        dma((SLOTS, 8)),
        dma((SLOTS, 8)),
        dma((2, 8)),
        dma((2, 8)),
        dma((SLOTS,)),
        dma((SLOTS,)),
        pltpu.SemaphoreType.REGULAR,
    ]
    outs = pl.pallas_call(
        functools.partial(kernel, nx, ny),
        out_shape=[jax.ShapeDtypeStruct(flat, f32)] * 2,
        in_specs=[pl.BlockSpec(memory_space=pltpu.HBM)] * 5,
        out_specs=[pl.BlockSpec(memory_space=pltpu.VMEM)] * 2,
        scratch_shapes=scratch,
        compiler_params=pltpu.CompilerParams(
            has_side_effects=True, collective_id=0, vmem_limit_bytes=48 * 1024 * 1024),
    )(disp.reshape(flat), vel.reshape(flat), load.reshape(flat), flags.reshape(cells, depth),
      mask_bits.reshape(words, cells, depth))
    return tuple(out.reshape(disp.shape) for out in outs)


def solution(mesh):
    cells = P(None, "gx", "gy", None)
    return jax.shard_map(
        functools.partial(on_device, mesh.shape["gx"], mesh.shape["gy"]),
        mesh=mesh,
        in_specs=(cells, cells, cells, P("gx", "gy", None), cells),
        out_specs=(cells, cells),
        check_vma=False,
    )
```

time: 77.5 us -> 59.9 us (0.77)
  Pallas kernels: 70.7 us -> 53.1 us
    pallas_call x1, Pallas kernels: 70.7 us -> 53.1 us  [on_device(): pl.pallas_call(functools.partial(kernel, nx, ny), out_shape=[jax.ShapeDty...]
where the time goes in v1:
time: 59.9 us; the launch traced here: 59.7 us
  Pallas kernels  53.1 us (89%)
  local copies, waits for them, and re-layouts  5.92 us (10%)
  between operations  0.65 us (1%)
    pallas_call x1, Pallas kernels, on_device(): pl.pallas_call(functools.partial(kernel, nx, ny), out_shape=[jax.ShapeDty...  53.1 us
    unnamed x12, local copies, waits for them, and re-layouts  5.92 us

profile of v1, /device:TPU:0, one launch (start us, length us, event | category | flops | bytes accessed | tf_op | source)
XLA Modules:
  0.0 59.7 jit_solution(1061097083334207030)
XLA Ops:
  0.6 0.0 copy-start
  0.6 0.9 %copy-done = s32[4,8,16,128]{3,2,1,0:T(8,128)S(1)} copy-done((s32[4,8,16,128]{3,2,1,0:T(8,128)S(1)}, s32[4,8,16,128]{3,2,1,0:T(8,128)}, u32[]{:S(2)}) %copy-start) | copy-done | bytes 262168
  1.6 0.0 copy-start.1
  1.6 0.9 %copy-done.1 = f32[3,8,16,128]{3,2,1,0:T(8,128)S(1)} copy-done((f32[3,8,16,128]{3,2,1,0:T(8,128)S(1)}, f32[3,8,16,128]{3,2,1,0:T(8,128)}, u32[]{:S(2)}) %copy-start.1) | copy-done | bytes 196632
  2.5 0.0 copy-start.2
  2.5 0.9 %copy-done.2 = f32[3,8,16,128]{3,2,1,0:T(8,128)S(1)} copy-done((f32[3,8,16,128]{3,2,1,0:T(8,128)S(1)}, f32[3,8,16,128]{3,2,1,0:T(8,128)}, u32[]{:S(2)}) %copy-start.2) | copy-done | bytes 196632
  3.4 0.0 copy-start.3
  3.4 0.9 %copy-done.3 = f32[3,8,16,128]{3,2,1,0:T(8,128)S(1)} copy-done((f32[3,8,16,128]{3,2,1,0:T(8,128)S(1)}, f32[3,8,16,128]{3,2,1,0:T(8,128)}, u32[]{:S(2)}) %copy-start.3) | copy-done | bytes 196632
  4.4 0.0 copy-start.4
  4.4 0.8 %copy-done.4 = s32[8,16,128]{2,1,0:T(8,128)S(1)} copy-done((s32[8,16,128]{2,1,0:T(8,128)S(1)}, s32[8,16,128]{2,1,0:T(8,128)}, u32[]{:S(2)}) %copy-start.4) | copy-done | bytes 65560
  5.2 53.1 %shard_map.68 = (f32[3,128,128]{2,1,0:T(8,128)S(1)}, f32[3,128,128]{2,1,0:T(8,128)S(1)}) custom-call(f32[3,128,128]{2,1,0:T(8,128)S(1)} %bitcast.8, f32[3,128,128]{2,1,0:T(8,128)S(1)} %bitcast.9, f32[3,128,128]{2,1,0:T(8,128)S(1)} %bitcast.10, s32[128,128]{1,0:T(8,128)S(1)} %bitcast.13, s32[4,128,128]{2,1,0:T(8,128)S(1)} %bitcast.7), custom_call_target="tpu_custom_call" | custom-call | tf_op jit(solution)/shard_map/pallas_call | solution.py:709
  58.3 0.7 %copy.9 = f32[3,8,16,128]{3,2,1,0:T(8,128)} copy(f32[3,8,16,128]{3,2,1,0:T(8,128)S(1)} %bitcast.12) | data formatting | bytes 393216
  59.0 0.7 %copy.10 = f32[3,8,16,128]{3,2,1,0:T(8,128)} copy(f32[3,8,16,128]{3,2,1,0:T(8,128)S(1)} %bitcast.11) | data formatting | bytes 393216
Async XLA Ops:
  0.6 1.0 %copy-start = (s32[4,8,16,128]{3,2,1,0:T(8,128)S(1)}, s32[4,8,16,128]{3,2,1,0:T(8,128)}, u32[]{:S(2)}) copy-start(s32[4,8,16,128]{3,2,1,0:T(8,128)} %param.9) | copy-start | bytes 786436
  1.6 0.9 %copy-start.1 = (f32[3,8,16,128]{3,2,1,0:T(8,128)S(1)}, f32[3,8,16,128]{3,2,1,0:T(8,128)}, u32[]{:S(2)}) copy-start(f32[3,8,16,128]{3,2,1,0:T(8,128)} %param.5) | copy-start | bytes 589828
  2.5 0.9 %copy-start.2 = (f32[3,8,16,128]{3,2,1,0:T(8,128)S(1)}, f32[3,8,16,128]{3,2,1,0:T(8,128)}, u32[]{:S(2)}) copy-start(f32[3,8,16,128]{3,2,1,0:T(8,128)} %param.6) | copy-start | bytes 589828
  3.4 0.9 %copy-start.3 = (f32[3,8,16,128]{3,2,1,0:T(8,128)S(1)}, f32[3,8,16,128]{3,2,1,0:T(8,128)}, u32[]{:S(2)}) copy-start(f32[3,8,16,128]{3,2,1,0:T(8,128)} %param.7) | copy-start | bytes 589828
  4.4 0.8 %copy-start.4 = (s32[8,16,128]{2,1,0:T(8,128)S(1)}, s32[8,16,128]{2,1,0:T(8,128)}, u32[]{:S(2)}) copy-start(s32[8,16,128]{2,1,0:T(8,128)} %param.8) | copy-start | bytes 196612

commit v2 on v1

--- a/solution.py
+++ b/solution.py
@@ -16,6 +16,7 @@
 
 EDGE = 8
 SLOTS = 4
+EARLY = 2
 
 
 def neighbour_table():
@@ -45,6 +46,7 @@
     return [(p, c) for c in range(-2, 3) for p in range(-2, 3) if far * far + p * p + c * c <= 9]
 
 
+SLOT = {(0, 0): 0, (0, 1): 1, (0, 2): 2, (1, 1): 3, (1, 2): 4, (2, 2): 5}
 FACE = {}
 for plane in PLANES:
     for offset in crossing(*plane):
@@ -92,7 +94,6 @@
     rows = pad.shape[1] - 6
     cols = cells // rows
     count = 3.0 * rows * nx * cols * ny * depth
-    devices = nx * ny
     my_x = lax.axis_index("gx")
     my_y = lax.axis_index("gy")
     f32, i32 = jnp.float32, jnp.int32
@@ -218,7 +219,22 @@
         for r in range(rows):
             mask_pad[word, 3 + r, pl.ds(EDGE, cols), :] = mask[word, pl.ds(r * cols, cols), :]
 
-    for along in range(-3, 4):
+    for side in range(2):
+        for layer in (1, 2):
+            at = layer - 1 if side == 0 else cols - layer
+            for word in range(4):
+                mypack[side, spread(4 * (layer - 1) + word), :] = mask[word, column(at), :]
+            at = layer - 1 if side == 0 else rows - layer
+            for word in range(4):
+                e = 4 * (layer - 1) + word
+                mxpack[side, pl.ds(e * cols, cols), :] = mask[word, pl.ds(at * cols, cols), :]
+        sign = 1 if side == 0 else -1
+        word = bond((0, 3 * sign, 0))[2]
+        my3pack[side] = mask[word, column(2 if side == 0 else cols - 3), :]
+        word = bond((3 * sign, 0, 0))[2]
+        mxpack[side, pl.ds(8 * cols, cols), :] = mask[word, pl.ds((2 if side == 0 else rows - 3) * cols, cols), :]
+
+    def own_weights(along):
         for word in range(4):
             mask_shifted[word] = mask_pad[word, :, pl.ds(EDGE + along, cols), :].reshape(-1, depth)
         for upward in range(-3, 4):
@@ -246,21 +262,8 @@
                     if scale and moments[power] is not None:
                         diagonal[slot, here] += scaled(scale, moments[power])
 
-    for side in range(2):
-        for layer in (1, 2):
-            at = layer - 1 if side == 0 else cols - layer
-            for word in range(4):
-                mypack[side, spread(4 * (layer - 1) + word), :] = mask[word, column(at), :]
-            at = layer - 1 if side == 0 else rows - layer
-            for word in range(4):
-                e = 4 * (layer - 1) + word
-                mxpack[side, pl.ds(e * cols, cols), :] = mask[word, pl.ds(at * cols, cols), :]
-        sign = 1 if side == 0 else -1
-        word = bond((0, 3 * sign, 0))[2]
-        my3pack[side] = mask[word, column(2 if side == 0 else cols - 3), :]
-        word = bond((3 * sign, 0, 0))[2]
-        mxpack[side, pl.ds(8 * cols, cols), :] = mask[word, pl.ds((2 if side == 0 else rows - 3) * cols, cols), :]
-
+    for along in range(-3, -3 + EARLY):
+        own_weights(along)
     pl.semaphore_wait(barrier, peers)
     for hop in range(1, ny):
         pl.semaphore_signal(ready, inc=1, device_id=(my_x, lax.rem(my_y + hop, ny)), device_id_type=MESH)
@@ -271,8 +274,8 @@
                 copy.start()
     fetches[1].wait()
     pack(field, 0)
-    fetches[2].wait()
-    pack(speed, 1)
+    for along in range(-3 + EARLY, 4):
+        own_weights(along)
 
     middle = (slice(None), pl.ds(3, rows), pl.ds(EDGE, cols), slice(None))
 
@@ -285,7 +288,7 @@
     def face_weights(side):
         sign = -1 if side == 0 else 1
         for axis in (0, 1):
-            terms = {}
+            terms, powers = {}, {}
             for layer, r in PLANES + LONG:
                 for p, c in crossing(layer, r) if (layer, r) in PLANES else [(0, 0)]:
                     out = sign * (layer + r)
@@ -310,14 +313,19 @@
                         wx[side, FACE[layer, r, p, c]] = one
                     else:
                         wy[side, FACE[layer, r, p, c]] = one
-                    slot = 0
-                    for i in range(3):
-                        for j in range(i, 3):
-                            scale = offset[i] * offset[j]
-                            if scale:
-                                key = (r, slot)
-                                terms[key] = add(terms.get(key), scaled(scale, one))
-                            slot += 1
+                    for power in range(3):
+                        if p**power:
+                            key = (out, r, c, power)
+                            powers[key] = add(powers.get(key), scaled(p**power, one))
+            for (out, r, c, power), term in powers.items():
+                for parts in ((0, 0), (0, 1), (0, 2), (1, 1), (1, 2), (2, 2)):
+                    tangent = 1 - axis
+                    if parts.count(tangent) != power:
+                        continue
+                    scale = out ** parts.count(axis) * c ** parts.count(2)
+                    if scale:
+                        key = (r, SLOT[parts])
+                        terms[key] = add(terms.get(key), scaled(scale, term))
             for (r, slot), term in terms.items():
                 if axis == 0:
                     at = r if side == 0 else rows - 1 - r
@@ -419,8 +427,7 @@
             force[1, here] -= d[1] * u[0] + d[3] * u[1] + d[4] * u[2]
             force[2, here] -= d[2] * u[0] + d[4] * u[1] + d[5] * u[2]
 
-    def face_forces(axis, side):
-        sign = -1 if side == 0 else 1
+    def face_forces(axis, side, sign):
         normal, tangent = (0, 1) if axis == 0 else (1, 0)
         result = {}
         for layer in (1, 2):
@@ -439,14 +446,14 @@
                             return xr[side, c + 2, e, pl.ds(EDGE + p, cols), :]
                         return yr[side, c + 2, spread((2 + p) * 8 + e), :]
 
-                    out = near(normal)
+                    out = sign * near(normal)
                     base = None
                     if p:
                         base = scaled(p, near(tangent))
                     if c:
                         base = add(base, scaled(c, near(2)))
                     for r in targets:
-                        value = scaled(sign * (layer + r), out)
+                        value = scaled(layer + r, out)
                         if base is not None:
                             value = value + base
                         one = (wx if axis == 0 else wy)[side, FACE[layer, r, p, c]] * value
@@ -462,7 +469,7 @@
                     if c:
                         wide[r, 2] = add(wide.get((r, 2)), scaled(c, sums[r, 0]))
             for r in inner:
-                wide[r, normal] = scaled(sign * (layer + r), wide[r, normal])
+                wide[r, normal] = sign * scaled(layer + r, wide[r, normal])
                 for component in range(3):
                     result[r, component] = add(result.get((r, component)), wide[r, component])
         for layer, r in LONG:
@@ -478,10 +485,11 @@
                 at = r if side == 0 else rows - 1 - r
                 force[component, pl.ds(at * cols, cols), :] += term
             else:
-                at = r if side == 0 else cols - 1 - r
+                at = jnp.where(side == 0, r, cols - 1 - r)
                 force[component, column(at), :] += term
 
-    me = my_x * ny + my_y
+    hops = [(hop_x, hop_y) for hop_y in range(ny) for hop_x in range(nx) if hop_x or hop_y]
+    hops.sort(key=lambda hop: (abs(2 * hop[1] - ny), abs(2 * hop[0] - nx)))
 
     def dot(first, second):
         whole = None
@@ -496,16 +504,12 @@
             line = jnp.where(place == which, one, line)
         sums_out[slot] = line
 
-        def send(r, carry):
-            target = lax.rem(me + 1 + r, devices)
+        for which, (hop_x, hop_y) in enumerate(hops):
             pltpu.make_async_remote_copy(
-                src_ref=sums_out.at[slot], dst_ref=sums_in.at[slot, r],
+                src_ref=sums_out.at[slot], dst_ref=sums_in.at[slot, which],
                 send_sem=sum_send_sem.at[slot], recv_sem=sum_recv_sem.at[slot],
-                device_id=(target // ny, lax.rem(target, ny)), device_id_type=MESH,
+                device_id=(lax.rem(my_x + hop_x, nx), lax.rem(my_y + hop_y, ny)), device_id_type=MESH,
             ).start()
-            return carry
-
-        lax.fori_loop(0, devices - 1, send, 0)
 
     def take_sums(slot):
         whole = sums_in.at[slot]
@@ -525,11 +529,15 @@
         ab[1:2, :] = jnp.broadcast_to(beta, (1, depth))
         return alpha, beta
 
+    near_side = 1 - lax.rem(my_y, 2)
+
     def step(turn, carry):
         own_forces()
 
         @pl.when(turn == 0)
         def _():
+            fetches[2].wait()
+            pack(speed, 1)
             take_masks()
 
         diagonal_forces()
@@ -567,23 +575,35 @@
                     xr[index, upward + 2, :, pl.ds(EDGE, cols), :] = rolled(
                         fresh[: 6 * cols], upward).reshape(6, cols, depth)
         for side in range(2):
-            face_forces(0, side)
-        for index in range(2, 8):
-            step_x, step_y, there = sides[index]
-
-            @pl.when(there)
-            def _():
-                arrived(index, slot)
-                side = 0 if step_y < 0 else 1
-                here = pl.ds(16, rows * 8) if index < 4 else pl.ds(0 if step_x < 0 else (rows + 2) * 8, 16)
-                fresh = alpha * yw[side, here] + beta * yslot[slot, side, here]
-                yw[side, here] = fresh
-                yg[side, here] = keep * yg[side, here] + fresh
-        for side in range(2):
+            face_forces(0, side, -1.0 if side == 0 else 1.0)
+        for side in (near_side, 1 - near_side):
+            step_y = 2 * side - 1
+            there_y = (my_y + step_y >= 0) & (my_y + step_y < ny)
+            for step_x in (0, -1, 1):
+                if step_x == 0:
+                    there, index, here = there_y, 2 + side, pl.ds(16, rows * 8)
+                    src = ypack.at[slot, side]
+                else:
+                    there = there_y & sides[0 if step_x < 0 else 1][2]
+                    index = (4 if step_x < 0 else 6) + side
+                    here = pl.ds(0 if step_x < 0 else (rows + 2) * 8, 16)
+                    src = ypack.at[slot, side, pl.ds(0, 16)]
+
+                @pl.when(there)
+                def _():
+                    copy = pltpu.make_async_remote_copy(
+                        src_ref=src, dst_ref=yslot.at[slot, side, here],
+                        send_sem=send_sem.at[slot, index], recv_sem=recv_sem.at[slot, index],
+                        device_id=(my_x + step_x, my_y + step_y), device_id_type=MESH,
+                    )
+                    copy.wait_send()
+                    copy.wait_recv()
+                    fresh = alpha * yw[side, here] + beta * yslot[slot, side, here]
+                    yw[side, here] = fresh
+                    yg[side, here] = keep * yg[side, here] + fresh
             for upward in range(-2, 3):
                 yr[side, upward + 2] = rolled(yg[side], upward)
-        for side in range(2):
-            face_forces(1, side)
+            face_forces(1, side, jnp.where(side == 0, -1.0, 1.0))
 
         @pl.when(turn == 0)
         def _():
@@ -713,7 +733,7 @@
         out_specs=[pl.BlockSpec(memory_space=pltpu.VMEM)] * 2,
         scratch_shapes=scratch,
         compiler_params=pltpu.CompilerParams(
-            has_side_effects=True, collective_id=0, vmem_limit_bytes=48 * 1024 * 1024),
+            has_side_effects=True, collective_id=0, vmem_limit_bytes=67043328),
     )(disp.reshape(flat), vel.reshape(flat), load.reshape(flat), flags.reshape(cells, depth),
       mask_bits.reshape(words, cells, depth))
     return tuple(out.reshape(disp.shape) for out in outs)

time: 59.9 us -> 53.6 us (0.89)
  local copies, waits for them, and re-layouts: 5.92 us -> 2.34 us
  Pallas kernels: 53.1 us -> 50.5 us
    unnamed x12 -> x4, local copies, waits for them, and re-layouts: 5.92 us -> 2.34 us
    pallas_call x1, Pallas kernels: 53.1 us -> 50.5 us  [on_device(): pl.pallas_call(functools.partial(kernel, nx, ny), out_shape=[jax.ShapeDty...]
where the time goes in v2:
time: 53.6 us; the launch traced here: 53.4 us
  Pallas kernels  50.5 us (94%)
  local copies, waits for them, and re-layouts  2.34 us (4%)
  between operations  0.65 us (1%)
    pallas_call x1, Pallas kernels, on_device(): pl.pallas_call(functools.partial(kernel, nx, ny), out_shape=[jax.ShapeDty...  50.5 us
    unnamed x4, local copies, waits for them, and re-layouts  2.34 us

profile of v2, /device:TPU:0, one launch (start us, length us, event | category | flops | bytes accessed | tf_op | source)
XLA Modules:
  0.0 53.4 jit_solution(9978655190328427231)
XLA Ops:
  0.6 50.5 %shard_map.68 = (f32[3,128,128]{2,1,0:T(8,128)}, f32[3,128,128]{2,1,0:T(8,128)}) custom-call(f32[3,128,128]{2,1,0:T(8,128)} %bitcast.8, f32[3,128,128]{2,1,0:T(8,128)} %bitcast.9, f32[3,128,128]{2,1,0:T(8,128)} %bitcast.10, s32[128,128]{1,0:T(8,128)} %bitcast.13, s32[4,128,128]{2,1,0:T(8,128)} %bitcast.7), custom_call_target="tpu_custom_call" | custom-call | tf_op jit(solution)/shard_map/pallas_call | solution.py:729
  51.1 0.0 copy-start
  51.1 1.7 %copy.9 = f32[3,8,16,128]{3,2,1,0:T(8,128)} copy(f32[3,8,16,128]{3,2,1,0:T(8,128)} %bitcast.12) | data formatting | bytes 393216
  52.8 0.0 copy-done
  52.8 0.7 %copy.10 = f32[3,8,16,128]{3,2,1,0:T(8,128)} copy(f32[3,8,16,128]{3,2,1,0:T(8,128)S(1)} %bitcast.11) | data formatting | bytes 393216
Async XLA Ops:
  51.1 1.7 %copy-start = (f32[3,128,128]{2,1,0:T(8,128)S(1)}, f32[3,128,128]{2,1,0:T(8,128)}, u32[]{:S(2)}) copy-start(f32[3,128,128]{2,1,0:T(8,128)} %get-tuple-element.5) | copy-start | bytes 589828

commit v3 on v2

--- a/solution.py
+++ b/solution.py
@@ -16,7 +16,8 @@
 
 EDGE = 8
 SLOTS = 4
-EARLY = 2
+EARLY = 3
+DEEP = 7
 
 
 def neighbour_table():
@@ -61,6 +62,12 @@
     mirror_word, mirror_bit = divmod(121 - number, 31)
     length = float(sum(part * part for part in offset))
     return word, 1 << bit, mirror_word, 1 << mirror_bit, 1.0 / (length * math.sqrt(length))
+
+
+FACE_WORDS = [
+    sorted({bond((sign * (layer + r), p, c))[2] for layer, r, p, c in FACE}) for sign in (-1, 1)
+]
+KEPT = max(len(words) for words in FACE_WORDS)
 
 
 def rolled(cells, upward):
@@ -136,13 +143,13 @@
         if index < 2:
             src, dst = xpack.at[slot, index], xslot.at[slot, 1 - index]
         elif index < 4:
-            src, dst = ypack.at[slot, index - 2], yslot.at[slot, 3 - index, pl.ds(2 * 8, rows * 8)]
+            src, dst = ypack.at[slot, index - 2], yslot.at[slot, 3 - index, pl.ds(2 * DEEP, rows * DEEP)]
         else:
             side = 0 if step_y < 0 else 1
             start = 0 if step_x < 0 else rows - 2
             land = rows + 2 if step_x < 0 else 0
-            src = ypack.at[slot, side, pl.ds(start * 8, 16)]
-            dst = yslot.at[slot, 1 - side, pl.ds(land * 8, 16)]
+            src = ypack.at[slot, side, pl.ds(start * DEEP, 2 * DEEP - 1)]
+            dst = yslot.at[slot, 1 - side, pl.ds(land * DEEP, 2 * DEEP - 1)]
         return pltpu.make_async_remote_copy(
             src_ref=src, dst_ref=dst, send_sem=send_sem.at[slot, index], recv_sem=recv_sem.at[slot, opposite(index)],
             device_id=(my_x + step_x, my_y + step_y), device_id_type=MESH,
@@ -176,30 +183,55 @@
     def column(at):
         return pl.ds(at, rows, stride=cols)
 
-    def spread(at):
-        return pl.ds(at, rows, stride=8)
-
-    def pack(source, slot):
-        for side in range(2):
-            for layer in (1, 2, 3):
-                at = layer - 1 if side == 0 else cols - layer
-                for c in range(3) if layer < 3 else (1,):
-                    e = 3 * (layer - 1) + (c if layer < 3 else 0)
-                    ypack[slot, side, spread(e), :] = source[c, column(at), :]
-        for index in ORDER[:6]:
-            @pl.when(sides[index][2])
+    def spread(at, deep=DEEP):
+        return pl.ds(at, rows, stride=deep)
+
+    def send_y(source, slot, side):
+        step_y = 2 * side - 1
+        there_y = (my_y + step_y >= 0) & (my_y + step_y < ny)
+        for layer in (1, 2, 3):
+            at = jnp.where(side == 0, layer - 1, cols - layer)
+            for c in range(3) if layer < 3 else (1,):
+                e = 3 * (layer - 1) + (c if layer < 3 else 0)
+                ypack[slot, side, spread(e), :] = source[c, column(at), :]
+        for step_x in (-1, 1, 0):
+            if step_x == 0:
+                there, index, other = there_y, 2 + side, 3 - side
+                src, dst = ypack.at[slot, side], yslot.at[slot, 1 - side, pl.ds(2 * DEEP, rows * DEEP)]
+            else:
+                there = there_y & sides[0 if step_x < 0 else 1][2]
+                index = (4 if step_x < 0 else 6) + side
+                other = 11 - index
+                start = 0 if step_x < 0 else rows - 2
+                land = rows + 2 if step_x < 0 else 0
+                src = ypack.at[slot, side, pl.ds(start * DEEP, 2 * DEEP - 1)]
+                dst = yslot.at[slot, 1 - side, pl.ds(land * DEEP, 2 * DEEP - 1)]
+
+            @pl.when(there)
             def _():
-                outgoing(index, slot).start()
+                pltpu.make_async_remote_copy(
+                    src_ref=src, dst_ref=dst, send_sem=send_sem.at[slot, index], recv_sem=recv_sem.at[slot, other],
+                    device_id=(my_x + step_x, my_y + step_y), device_id_type=MESH,
+                ).start()
+
+    def send_x(source, slot):
         for side in range(2):
             for layer in (1, 2, 3):
                 at = layer - 1 if side == 0 else rows - layer
                 for c in range(3) if layer < 3 else (0,):
                     e = 3 * (layer - 1) + c
                     xpack[slot, side, pl.ds(e * cols, cols), :] = source[c, pl.ds(at * cols, cols), :]
-        for index in ORDER[6:]:
+        for index in (0, 1):
             @pl.when(sides[index][2])
             def _():
                 outgoing(index, slot).start()
+
+    near_side = 1 - lax.rem(my_y, 2)
+
+    def pack(source, slot):
+        send_y(source, slot, 1 - near_side)
+        send_y(source, slot, near_side)
+        send_x(source, slot)
 
     def arrived(index, slot):
         outgoing(index, slot).wait_send()
@@ -223,16 +255,16 @@
         for layer in (1, 2):
             at = layer - 1 if side == 0 else cols - layer
             for word in range(4):
-                mypack[side, spread(4 * (layer - 1) + word), :] = mask[word, column(at), :]
+                mypack[side, spread(4 * (layer - 1) + word, 8), :] = mask[word, column(at), :]
             at = layer - 1 if side == 0 else rows - layer
-            for word in range(4):
-                e = 4 * (layer - 1) + word
+            for kept, word in enumerate(FACE_WORDS[1 - side]):
+                e = KEPT * (layer - 1) + kept
                 mxpack[side, pl.ds(e * cols, cols), :] = mask[word, pl.ds(at * cols, cols), :]
         sign = 1 if side == 0 else -1
         word = bond((0, 3 * sign, 0))[2]
         my3pack[side] = mask[word, column(2 if side == 0 else cols - 3), :]
         word = bond((3 * sign, 0, 0))[2]
-        mxpack[side, pl.ds(8 * cols, cols), :] = mask[word, pl.ds((2 if side == 0 else rows - 3) * cols, cols), :]
+        mxpack[side, pl.ds(2 * KEPT * cols, cols), :] = mask[word, pl.ds((2 if side == 0 else rows - 3) * cols, cols), :]
 
     def own_weights(along):
         for word in range(4):
@@ -274,6 +306,8 @@
                 copy.start()
     fetches[1].wait()
     pack(field, 0)
+    fetches[2].wait()
+    pack(speed, 1)
     for along in range(-3 + EARLY, 4):
         own_weights(along)
 
@@ -282,60 +316,57 @@
     def set_pad(c, value):
         pad[c, pl.ds(3, rows), pl.ds(EDGE, cols), :] = value.reshape(rows, cols, depth)
 
-    for c in range(3):
-        set_pad(c, field[c])
-
-    def face_weights(side):
+    def face_weights(axis, side):
         sign = -1 if side == 0 else 1
-        for axis in (0, 1):
-            terms, powers = {}, {}
-            for layer, r in PLANES + LONG:
-                for p, c in crossing(layer, r) if (layer, r) in PLANES else [(0, 0)]:
-                    out = sign * (layer + r)
-                    offset = (out, p, c) if axis == 0 else (p, out, c)
-                    word, bit, mirror_word, mirror_bit, weight = bond(offset)
-                    if axis == 0:
-                        at = r if side == 0 else rows - 1 - r
-                        own = mask[word, pl.ds(at * cols, cols), :]
-                        if layer == 3:
-                            far = mx3[side]
-                        else:
-                            far = mxr[side, c + 2, 4 * (layer - 1) + mirror_word, pl.ds(EDGE + p, cols), :]
-                    else:
-                        at = r if side == 0 else cols - 1 - r
-                        own = mask[word, column(at), :]
-                        if layer == 3:
-                            far = my3[side]
-                        else:
-                            far = myr[side, c + 2, spread((2 + p) * 8 + 4 * (layer - 1) + mirror_word), :]
-                    one = jnp.where(((own & bit) | (far & mirror_bit)) == 0, f32(weight), f32(0.0))
-                    if axis == 0:
-                        wx[side, FACE[layer, r, p, c]] = one
-                    else:
-                        wy[side, FACE[layer, r, p, c]] = one
-                    for power in range(3):
-                        if p**power:
-                            key = (out, r, c, power)
-                            powers[key] = add(powers.get(key), scaled(p**power, one))
-            for (out, r, c, power), term in powers.items():
-                for parts in ((0, 0), (0, 1), (0, 2), (1, 1), (1, 2), (2, 2)):
-                    tangent = 1 - axis
-                    if parts.count(tangent) != power:
-                        continue
-                    scale = out ** parts.count(axis) * c ** parts.count(2)
-                    if scale:
-                        key = (r, SLOT[parts])
-                        terms[key] = add(terms.get(key), scaled(scale, term))
-            for (r, slot), term in terms.items():
+        terms, powers = {}, {}
+        for layer, r in PLANES + LONG:
+            for p, c in crossing(layer, r) if (layer, r) in PLANES else [(0, 0)]:
+                out = sign * (layer + r)
+                offset = (out, p, c) if axis == 0 else (p, out, c)
+                word, bit, mirror_word, mirror_bit, weight = bond(offset)
                 if axis == 0:
                     at = r if side == 0 else rows - 1 - r
-                    diagonal[slot, pl.ds(at * cols, cols), :] += term
+                    own = mask[word, pl.ds(at * cols, cols), :]
+                    if layer == 3:
+                        far = mx3[side]
+                    else:
+                        kept = KEPT * (layer - 1) + FACE_WORDS[side].index(mirror_word)
+                        far = mxr[side, c + 2, kept, pl.ds(EDGE + p, cols), :]
                 else:
                     at = r if side == 0 else cols - 1 - r
-                    diagonal[slot, column(at), :] += term
-
-    def take_masks():
-        for index in range(8):
+                    own = mask[word, column(at), :]
+                    if layer == 3:
+                        far = my3[side]
+                    else:
+                        far = myr[side, c + 2, spread((2 + p) * 8 + 4 * (layer - 1) + mirror_word, 8), :]
+                one = jnp.where(((own & bit) | (far & mirror_bit)) == 0, f32(weight), f32(0.0))
+                if axis == 0:
+                    wx[side, FACE[layer, r, p, c]] = one
+                else:
+                    wy[side, FACE[layer, r, p, c]] = one
+                for power in range(3):
+                    if p**power:
+                        key = (out, r, c, power)
+                        powers[key] = add(powers.get(key), scaled(p**power, one))
+        for (out, r, c, power), term in powers.items():
+            for parts in ((0, 0), (0, 1), (0, 2), (1, 1), (1, 2), (2, 2)):
+                tangent = 1 - axis
+                if parts.count(tangent) != power:
+                    continue
+                scale = out ** parts.count(axis) * c ** parts.count(2)
+                if scale:
+                    key = (r, SLOT[parts])
+                    terms[key] = add(terms.get(key), scaled(scale, term))
+        for (r, slot), term in terms.items():
+            if axis == 0:
+                at = r if side == 0 else rows - 1 - r
+                diagonal[slot, pl.ds(at * cols, cols), :] += term
+            else:
+                at = r if side == 0 else cols - 1 - r
+                diagonal[slot, column(at), :] += term
+
+    def take_masks(axis):
+        for index in range(2) if axis == 0 else range(2, 8):
             step_x, step_y, there = sides[index]
 
             @pl.when(there)
@@ -347,7 +378,7 @@
                 for upward in range(-2, 3):
                     inside = (place + upward >= 0) & (place + upward < depth)
                     if index < 2:
-                        words = mxslot[index, pl.ds(0, 8 * cols), :]
+                        words = mxslot[index, pl.ds(0, 2 * KEPT * cols), :]
                     elif index < 4:
                         first, size = 2 * 8, rows * 8
                         words = myslot[index - 2, pl.ds(first, size), :]
@@ -357,15 +388,15 @@
                     if upward:
                         words = jnp.where(inside, rolled(words, upward), -1)
                     if index < 2:
-                        mxr[index, upward + 2, :, pl.ds(EDGE, cols), :] = words.reshape(8, cols, depth)
+                        mxr[index, upward + 2, :, pl.ds(EDGE, cols), :] = words.reshape(2 * KEPT, cols, depth)
                     else:
                         myr[0 if step_y < 0 else 1, upward + 2, pl.ds(first, size), :] = words
                 if index < 2:
-                    mx3[index] = mxslot[index, pl.ds(8 * cols, cols), :]
+                    mx3[index] = mxslot[index, pl.ds(2 * KEPT * cols, cols), :]
                 elif index < 4:
                     my3[index - 2] = my3slot[index - 2]
         for side in range(2):
-            face_weights(side)
+            face_weights(axis, side)
 
     def own_forces():
         turn = 0
@@ -444,7 +475,7 @@
                         e = 3 * (layer - 1) + component
                         if axis == 0:
                             return xr[side, c + 2, e, pl.ds(EDGE + p, cols), :]
-                        return yr[side, c + 2, spread((2 + p) * 8 + e), :]
+                        return yr[side, c + 2, spread((2 + p) * DEEP + e), :]
 
                     out = sign * near(normal)
                     base = None
@@ -477,7 +508,7 @@
             if axis == 0:
                 out = xg[side, pl.ds(e * cols, cols), :]
             else:
-                out = yg[side, spread(2 * 8 + e), :]
+                out = yg[side, spread(2 * DEEP + e), :]
             one = 9.0 * ((wx if axis == 0 else wy)[side, FACE[layer, r, 0, 0]] * out)
             result[r, normal] = add(result.get((r, normal)), one)
         for (r, component), term in result.items():
@@ -529,19 +560,21 @@
         ab[1:2, :] = jnp.broadcast_to(beta, (1, depth))
         return alpha, beta
 
-    near_side = 1 - lax.rem(my_y, 2)
-
     def step(turn, carry):
-        own_forces()
+        @pl.when(turn != 1)
+        def _():
+            own_forces()
 
         @pl.when(turn == 0)
         def _():
-            fetches[2].wait()
-            pack(speed, 1)
-            take_masks()
-
-        diagonal_forces()
-
+            take_masks(0)
+
+        @pl.when(turn == 1)
+        def _():
+            for c in range(3):
+                force[c] = change[c]
+
+        sent = lax.rem(turn + 2, SLOTS)
         slot = jnp.where(turn < 3, turn, lax.rem(turn + 1, SLOTS))
         early = turn < 3
         alpha = jnp.where(early, 0.0, ab[0:1, :])
@@ -560,7 +593,7 @@
                         xw[index] = xslot[3, index]
                     else:
                         side = 0 if step_y < 0 else 1
-                        here = pl.ds(16, rows * 8) if index < 4 else pl.ds(0 if step_x < 0 else (rows + 2) * 8, 16)
+                        here = pl.ds(2 * DEEP, rows * DEEP) if index < 4 else pl.ds(0 if step_x < 0 else (rows + 2) * DEEP, 2 * DEEP - 1)
                         yw[side, here] = yslot[3, side, here]
 
         for index in (0, 1):
@@ -576,18 +609,32 @@
                         fresh[: 6 * cols], upward).reshape(6, cols, depth)
         for side in range(2):
             face_forces(0, side, -1.0 if side == 0 else 1.0)
+
+        @pl.when(turn == 0)
+        def _():
+            take_masks(1)
+
+        diagonal_forces()
+
+        @pl.when(turn == 0)
+        def _():
+            fetches[3].wait()
+            fetches[4].wait()
+            for c in range(3):
+                force[c] += flags[...].astype(f32) * load[c]
+
         for side in (near_side, 1 - near_side):
             step_y = 2 * side - 1
             there_y = (my_y + step_y >= 0) & (my_y + step_y < ny)
             for step_x in (0, -1, 1):
                 if step_x == 0:
-                    there, index, here = there_y, 2 + side, pl.ds(16, rows * 8)
+                    there, index, here = there_y, 2 + side, pl.ds(2 * DEEP, rows * DEEP)
                     src = ypack.at[slot, side]
                 else:
                     there = there_y & sides[0 if step_x < 0 else 1][2]
                     index = (4 if step_x < 0 else 6) + side
-                    here = pl.ds(0 if step_x < 0 else (rows + 2) * 8, 16)
-                    src = ypack.at[slot, side, pl.ds(0, 16)]
+                    here = pl.ds(0 if step_x < 0 else (rows + 2) * DEEP, 2 * DEEP - 1)
+                    src = ypack.at[slot, side, pl.ds(0, 2 * DEEP - 1)]
 
                 @pl.when(there)
                 def _():
@@ -605,22 +652,18 @@
                 yr[side, upward + 2] = rolled(yg[side], upward)
             face_forces(1, side, jnp.where(side == 0, -1.0, 1.0))
 
+            @pl.when(turn < ITERS)
+            def _():
+                send_y(force, sent, side)
+
+        @pl.when(turn < ITERS)
+        def _():
+            send_x(force, sent)
+
         @pl.when(turn == 0)
         def _():
-            fetches[3].wait()
-            fetches[4].wait()
             for c in range(3):
-                whole = force[c] + flags[...].astype(f32) * load[c]
-                force[c] = whole
-                total[c] = whole
-
-        @pl.when(turn < ITERS)
-        def _():
-            pack(force, lax.rem(turn + 2, SLOTS))
-
-        @pl.when(turn == 0)
-        def _():
-            for c in range(3):
+                total[c] = force[c]
                 set_pad(c, speed[c])
 
         @pl.when(turn == 1)
@@ -658,6 +701,12 @@
 
         return carry
 
+    for c in range(3):
+        set_pad(c, speed[c])
+    own_forces()
+    for c in range(3):
+        change[c] = force[c]
+        set_pad(c, field[c])
     lax.fori_loop(0, ITERS + 1, step, 0)
     alpha, beta = take_sums((ITERS - 1) % SLOTS)
     for c in range(3):
@@ -676,6 +725,7 @@
     flat = (parts, cells, depth)
     tall = (rows + 6) * cols
     ring = (rows + 4) * 8
+    deep = (rows + 4) * DEEP
     scratch = [
         vmem(flat, f32),
         vmem((cells, depth), i32),
@@ -695,22 +745,22 @@
         vmem((2, len(FACE), rows, depth), f32),
         vmem((2, 7 * cols, depth), f32),
         vmem((2, 7 * cols, depth), f32),
-        vmem((2, ring, depth), f32),
-        vmem((2, ring, depth), f32),
+        vmem((2, deep, depth), f32),
+        vmem((2, deep, depth), f32),
         vmem((2, 5, 6, wide, depth), f32),
-        vmem((2, 5, ring, depth), f32),
-        vmem((2, 5, 8, wide, depth), i32),
+        vmem((2, 5, deep, depth), f32),
+        vmem((2, 5, 2 * KEPT, wide, depth), i32),
         vmem((2, 5, ring, depth), i32),
         vmem((2, cols, depth), i32),
         vmem((2, rows, depth), i32),
         vmem((SLOTS, 2, 7 * cols, depth), f32),
-        vmem((SLOTS, 2, rows * 8, depth), f32),
+        vmem((SLOTS, 2, rows * DEEP, depth), f32),
         vmem((SLOTS, 2, 7 * cols, depth), f32),
-        vmem((SLOTS, 2, ring, depth), f32),
-        vmem((2, 9 * cols, depth), i32),
+        vmem((SLOTS, 2, deep, depth), f32),
+        vmem((2, (2 * KEPT + 1) * cols, depth), i32),
         vmem((2, rows * 8, depth), i32),
         vmem((2, rows, depth), i32),
-        vmem((2, 9 * cols, depth), i32),
+        vmem((2, (2 * KEPT + 1) * cols, depth), i32),
         vmem((2, ring, depth), i32),
         vmem((2, rows, depth), i32),
         vmem((6, 8, depth), f32),

time: 53.6 us -> 51.6 us (0.963)
  Pallas kernels: 50.5 us -> 48.5 us
    pallas_call x1, Pallas kernels: 50.5 us -> 48.5 us  [on_device(): pl.pallas_call(functools.partial(kernel, nx, ny), out_shape=[jax.ShapeDty...]
where the time goes in v3:
time: 51.6 us; the launch traced here: 51.5 us
  Pallas kernels  48.5 us (94%)
  local copies, waits for them, and re-layouts  2.34 us (5%)
  between operations  0.65 us (1%)
    pallas_call x1, Pallas kernels, on_device(): pl.pallas_call(functools.partial(kernel, nx, ny), out_shape=[jax.ShapeDty...  48.5 us
    unnamed x4, local copies, waits for them, and re-layouts  2.34 us

profile of v3, /device:TPU:0, one launch (start us, length us, event | category | flops | bytes accessed | tf_op | source)
XLA Modules:
  0.0 51.5 jit_solution(6527926878560737267)
XLA Ops:
  0.6 48.5 %shard_map.68 = (f32[3,128,128]{2,1,0:T(8,128)}, f32[3,128,128]{2,1,0:T(8,128)}) custom-call(f32[3,128,128]{2,1,0:T(8,128)} %bitcast.8, f32[3,128,128]{2,1,0:T(8,128)} %bitcast.9, f32[3,128,128]{2,1,0:T(8,128)} %bitcast.10, s32[128,128]{1,0:T(8,128)} %bitcast.13, s32[4,128,128]{2,1,0:T(8,128)} %bitcast.7), custom_call_target="tpu_custom_call" | custom-call | tf_op jit(solution)/shard_map/pallas_call | solution.py:779
  49.1 0.0 copy-start
  49.1 1.7 %copy.9 = f32[3,8,16,128]{3,2,1,0:T(8,128)} copy(f32[3,8,16,128]{3,2,1,0:T(8,128)} %bitcast.12) | data formatting | bytes 393216
  50.8 0.0 copy-done
  50.8 0.7 %copy.10 = f32[3,8,16,128]{3,2,1,0:T(8,128)} copy(f32[3,8,16,128]{3,2,1,0:T(8,128)S(1)} %bitcast.11) | data formatting | bytes 393216
Async XLA Ops:
  49.1 1.7 %copy-start = (f32[3,128,128]{2,1,0:T(8,128)S(1)}, f32[3,128,128]{2,1,0:T(8,128)}, u32[]{:S(2)}) copy-start(f32[3,128,128]{2,1,0:T(8,128)} %get-tuple-element.5) | copy-start | bytes 589828

commit v4 on v3

--- a/solution.py
+++ b/solution.py
@@ -16,7 +16,7 @@
 
 EDGE = 8
 SLOTS = 4
-EARLY = 3
+EARLY = 4
 DEEP = 7
 
 

time: 51.6 us -> 51.8 us (level)
  no operation moved by 1% of the time
where the time goes in v4:
time: 51.8 us; the launch traced here: 51.6 us
  Pallas kernels  48.6 us (94%)
  local copies, waits for them, and re-layouts  2.34 us (5%)
  between operations  0.65 us (1%)
    pallas_call x1, Pallas kernels, on_device(): pl.pallas_call(functools.partial(kernel, nx, ny), out_shape=[jax.ShapeDty...  48.6 us
    unnamed x4, local copies, waits for them, and re-layouts  2.34 us

profile of v4, /device:TPU:0, one launch (start us, length us, event | category | flops | bytes accessed | tf_op | source)
XLA Modules:
  0.0 51.6 jit_solution(18234753247951649189)
XLA Ops:
  0.6 48.6 %shard_map.68 = (f32[3,128,128]{2,1,0:T(8,128)}, f32[3,128,128]{2,1,0:T(8,128)}) custom-call(f32[3,128,128]{2,1,0:T(8,128)} %bitcast.8, f32[3,128,128]{2,1,0:T(8,128)} %bitcast.9, f32[3,128,128]{2,1,0:T(8,128)} %bitcast.10, s32[128,128]{1,0:T(8,128)} %bitcast.13, s32[4,128,128]{2,1,0:T(8,128)} %bitcast.7), custom_call_target="tpu_custom_call" | custom-call | tf_op jit(solution)/shard_map/pallas_call | solution.py:779
  49.3 0.0 copy-start
  49.3 1.7 %copy.9 = f32[3,8,16,128]{3,2,1,0:T(8,128)} copy(f32[3,8,16,128]{3,2,1,0:T(8,128)} %bitcast.12) | data formatting | bytes 393216
  50.9 0.0 copy-done
  50.9 0.7 %copy.10 = f32[3,8,16,128]{3,2,1,0:T(8,128)} copy(f32[3,8,16,128]{3,2,1,0:T(8,128)S(1)} %bitcast.11) | data formatting | bytes 393216
Async XLA Ops:
  49.3 1.7 %copy-start = (f32[3,128,128]{2,1,0:T(8,128)S(1)}, f32[3,128,128]{2,1,0:T(8,128)}, u32[]{:S(2)}) copy-start(f32[3,128,128]{2,1,0:T(8,128)} %get-tuple-element.5) | copy-start | bytes 589828
